TPU v7x, 32 devices: a whole 2x2x4 slice. The times are simulated.
32 devices in a mesh: pix: 32 (over z, y, x, core).
Axes of the slice: x: 2, y: 2, z: 4, core: 2. Of those that a mesh axis runs over, the one named last changes fastest.
Arguments:
- green: float32 [2048, 6144], P('pix'), may hold values from -200 to 200, as said below
- sketch: float32 [6144, 128], P('pix'), may hold values from -0.078125 to 0.078125
Outputs:
- basis: float32 [2048, 128], P('pix')
- projection: float32 [6144, 128], P('pix')
- spectrum_gram: float32 [128, 128], replicated
Inputs may be any that keep to these rules, and one draw needn't show every extreme that they name: `green`: finite real entries; each patch's column has its own scale.
All inputs are finite; a program needn't handle non-finite values.
Results may differ from a plain program's by a relative error of at most 0.000086.
Values sent between devices are 32-bit elements; how exact they have to be, the bound alone decides.
No kernel may reach another device: no remote copies, remote signals or barrier semaphores. Data moves between devices by JAX's collectives and lax.ppermute only.
A program may use at most 64 MiB of HBM per device.

v0:
```python
import jax
import jax.numpy as jnp
from jax import lax
from jax.sharding import PartitionSpec as P

PATCHES = 6144


def body(green, sketch):
    highest = lax.Precision.HIGHEST
    rows_here = green.shape[0]
    devices_pix = lax.axis_size("pix")
    total_pixels = rows_here * devices_pix
    columns = green
    sketched = jnp.dot(
        columns,
        lax.all_gather(sketch, "pix", axis=0, tiled=True),
        precision=highest,
        preferred_element_type=jnp.float32,
    )
    local_gram = jnp.dot(
        sketched.T, sketched, precision=highest, preferred_element_type=jnp.float32
    )
    columns = green
    raw_proj = lax.psum_scatter(
        lax.dot_general(
            columns,
            sketched,
            (((0,), (0,)), ((), ())),
            precision=highest,
            preferred_element_type=jnp.float32,
        ),
        "pix",
        scatter_dimension=0,
        tiled=True,
    )
    gram = lax.psum(local_gram, "pix")
    lower = jnp.linalg.cholesky(gram)
    orthonormal = jax.scipy.linalg.solve_triangular(lower, sketched.T, lower=True).T
    projection = jax.scipy.linalg.solve_triangular(lower, raw_proj.T, lower=True).T
    basis = jnp.sqrt(jnp.float32(total_pixels)) * orthonormal
    local_spec = jnp.dot(
        projection.T, projection, precision=highest, preferred_element_type=jnp.float32
    )
    spectrum_gram = lax.psum(local_spec, "pix") / jnp.float32(PATCHES)
    return (basis, projection, spectrum_gram)


def solution(mesh):
    in_specs = (P("pix", None), P("pix", None))
    out_specs = (P("pix", None), P("pix", None), P())
    return jax.shard_map(body, mesh=mesh, in_specs=in_specs, out_specs=out_specs, check_vma=False)
```

profile of v0, /device:TPU:1, one launch (start us, length us, event | category | flops | bytes accessed | tf_op | source)
XLA Modules:
  0.0 439.5 jit_solution(5103394524616839399)
XLA Ops:
  7.2 0.0 copy-start
  7.2 0.0 all-gather.2.cloned.1.call-start
  7.2 0.7 all-gather.2.cloned.1.call-update
  7.9 0.0 all-reduce.3.cloned.1.call-start
  8.0 64.5 %all-gather.2.cloned.1.call-done = f32[6144,128]{1,0:T(8,128)} async-done(((f32[192,128]{1,0:T(8,128)}), f32[6144,128]{1,0:T(8,128)}) %all-gather.2.cloned.1.call-update) | async-done | bytes 3145744 | tf_op jit(solution)/shard_map/all_gather | solution.py:17
  72.4 0.0 copy-done
  72.4 3.9 fusion.5
  76.3 0.9 fusion.6
  77.3 0.0 all-reduce.3.cloned.1.call-update
  77.3 0.0 reduce-scatter.4.cloned.1.call-start
  77.3 4.4 convolution_bitcast_fusion
  81.7 3.6 copy.10
  85.2 0.0 reduce-scatter.4.cloned.1.call-update
  85.3 0.2 all-reduce.5.cloned.1.call-start
  85.5 112.7 %all-reduce.3.cloned.1.call-done = f32[128,128]{0,1:T(8,128)} async-done(((f32[128,128]{0,1:T(8,128)}), f32[128,128]{0,1:T(8,128)}) %all-reduce.3.cloned.1.call-update) | async-done | bytes 65552 | tf_op jit(solution)/shard_map/psum | solution.py:37
  198.2 0.9 copy.8
  199.1 0.9 fusion.4
  200.0 11.7 %cholesky.16 = f32[128,128]{1,0:T(8,128)S(1)} custom-call(f32[128,128]{1,0:T(8,128)S(1)} %fusion.4), custom_call_target="Cholesky" | custom-call | tf_op jit(solution)/shard_map/jit(cholesky)/cholesky | solution.py:38
  211.7 0.6 compare_reduce_fusion
  212.4 0.7 fusion
  213.0 9.8 %custom-call.10 = f32[1,128,128]{1,2,0:T(8,128)S(1)} custom-call(f32[1,128,128]{2,1,0:T(8,128)S(1)} %fusion), custom_call_target="InvertDiagBlocksLowerTriangular" | custom-call | tf_op jit(solution)/shard_map/jit(_solve_triangular)/triangular_solve | solution.py:39
  222.9 80.8 %reduce-scatter.4.cloned.1.call-done = f32[192,128]{1,0:T(8,128)} async-done(((f32[6144,128]{1,0:T(8,128)}), f32[192,128]{1,0:T(8,128)}) %reduce-scatter.4.cloned.1.call-update) | async-done | bytes 98320
  303.6 1.1 fusion.1
  304.8 0.0 copy-start.1
  304.8 1.1 fusion.7
  305.9 0.0 all-reduce.5.cloned.1.call-update
  305.9 0.8 convolution_multiply_fusion
  306.7 124.8 %all-reduce.5.cloned.1.call-done = f32[128,128]{1,0:T(8,128)} async-done(((f32[128,128]{1,0:T(8,128)}), f32[128,128]{1,0:T(8,128)}) %all-reduce.5.cloned.1.call-update) | async-done | bytes 65552 | tf_op jit(solution)/shard_map/psum | solution.py:45
  431.5 1.5 broadcast_multiply_fusion
  433.0 0.0 copy-done.1
  (1 shorter events, 0.0 us)
Async XLA Ops:
  7.2 65.3 %copy-start = (f32[64,6144]{1,0:T(8,128)S(1)}, f32[64,6144]{1,0:T(8,128)}, u32[]{:S(2)}) copy-start(f32[64,6144]{1,0:T(8,128)} %param.2) | copy-start | bytes 4718596
  7.2 65.2 %all-gather.2.cloned.1.call-start = ((), (), s32[]{:S(2)}) async-start(), calls=%async_computation.1 | async-start | bytes 3244032 | tf_op jit(solution)/shard_map/all_gather | solution.py:17
  7.9 190.3 %all-reduce.3.cloned.1.call-start = ((), (), s32[]{:S(2)}) async-start(), calls=%async_computation.2 | async-start | bytes 131072 | tf_op jit(solution)/shard_map/psum | solution.py:37
  77.3 226.4 %reduce-scatter.4.cloned.1.call-start = ((), (), s32[]{:S(2)}) async-start(), calls=%async_computation.4 | async-start | bytes 3244032
  85.3 346.3 %all-reduce.5.cloned.1.call-start = ((), (), s32[]{:S(2)}) async-start(), calls=%async_computation.3 | async-start | bytes 131072 | tf_op jit(solution)/shard_map/psum | solution.py:45
  304.8 128.2 %copy-start.1 = (f32[128,192]{0,1:T(8,128)}, f32[128,192]{0,1:T(8,128)S(1)}, u32[]{:S(2)}) copy-start(f32[128,192]{0,1:T(8,128)S(1)} %fusion.1) | copy-start | bytes 294916
Sparse Core Ops, SparseCore 0:
  10.9 61.5 all-gather.1
  78.6 119.5 all-reduce.2
  203.6 99.9 reduce-scatter.3
  309.6 121.8 all-reduce.4
where the time goes:
time: 440 us
  waiting for transfers between devices  384 us (87%)
  other arithmetic  25.2 us (6%)
  between operations  13.8 us (3%)
  matrix products  12.2 us (3%)
  local copies, waits for them, and re-layouts  4.5 us (1%)
    psum x1, waiting for transfers between devices, body(): spectrum_gram = lax.psum(local_spec, 'pix') / jnp.float32(PATCHES)  125 us
    psum x1, waiting for transfers between devices, body(): gram = lax.psum(local_gram, 'pix')  113 us
    unnamed x5, waiting for transfers between devices  81.5 us
    all_gather x1, waiting for transfers between devices, body(): lax.all_gather(sketch, 'pix', axis=0, tiled=True)  64.5 us
    another operation x3, other arithmetic, body(): lower = jnp.linalg.cholesky(gram)  12.4 us
    another operation x2, other arithmetic, body(): jax.scipy.linalg.solve_triangular(lower, sketched.T, lower=True)  10.5 us
  transfers between devices with their start and end apart: 4, of which 4 were waited for; matrix products, arithmetic and copies ran while one was open for 8% of the time, Pallas kernels for 0%

commit v1 on v0

--- a/solution.py
+++ b/solution.py
@@ -1,9 +1,18 @@
+import functools
 import jax
 import jax.numpy as jnp
 from jax import lax
 from jax.sharding import PartitionSpec as P
 
 PATCHES = 6144
+
+
+def serve_screen_on_mesh(state, mesh_name):
+    z2 = lax.all_gather(state, mesh_name).sum(axis=0)
+    return z2
+
+
+part_sample_here = functools.partial(serve_screen_on_mesh, mesh_name="pix")
 
 
 def body(green, sketch):
@@ -42,7 +51,7 @@
     local_spec = jnp.dot(
         projection.T, projection, precision=highest, preferred_element_type=jnp.float32
     )
-    spectrum_gram = lax.psum(local_spec, "pix") / jnp.float32(PATCHES)
+    spectrum_gram = part_sample_here(local_spec) / jnp.float32(PATCHES)
     return (basis, projection, spectrum_gram)
 
 

time: 440 us -> 374 us (0.85)
  waiting for transfers between devices: 384 us -> 316 us
    psum x1 -> x0, waiting for transfers between devices: 125 us -> none  [body(): spectrum_gram = lax.psum(local_spec, 'pix') / jnp.float32(PATCHES)]
    all_gather x0 -> x1, waiting for transfers between devices: none -> 57.6 us  [serve_screen_on_mesh(): z2 = lax.all_gather(state, mesh_name).sum(axis=0)]
  transfers between devices with their start and end apart: 4 -> 4, of which waited for: 4 -> 4; matrix products, arithmetic and copies ran while one was open for 8% -> 9% of each run, Pallas kernels for 0% -> 0%
where the time goes in v1:
time: 374 us; the launch traced here: 373 us
  waiting for transfers between devices  316 us (84%)
  other arithmetic  26.1 us (7%)
  between operations  13.8 us (4%)
  matrix products  12.2 us (3%)
  local copies, waits for them, and re-layouts  4.5 us (1%)
    psum x1, waiting for transfers between devices, body(): gram = lax.psum(local_gram, 'pix')  113 us
    unnamed x5, waiting for transfers between devices  81.5 us
    all_gather x1, waiting for transfers between devices, body(): lax.all_gather(sketch, 'pix', axis=0, tiled=True)  64.5 us
    all_gather x1, waiting for transfers between devices, serve_screen_on_mesh(): z2 = lax.all_gather(state, mesh_name).sum(axis=0)  57.6 us
    another operation x3, other arithmetic, body(): lower = jnp.linalg.cholesky(gram)  12.4 us
    another operation x2, other arithmetic, body(): jax.scipy.linalg.solve_triangular(lower, sketched.T, lower=True)  10.5 us
  transfers between devices with their start and end apart: 4, of which 4 were waited for; matrix products, arithmetic and copies ran while one was open for 9% of the time, Pallas kernels for 0%

profile of v1, /device:TPU:1, one launch (start us, length us, event | category | flops | bytes accessed | tf_op | source)
XLA Modules:
  0.0 373.1 jit_solution(11456021701532989510)
XLA Ops:
  7.2 0.0 copy-start
  7.2 0.0 all-gather.4.cloned.1.call-start
  7.2 0.7 all-gather.4.cloned.1.call-update
  7.9 0.0 all-reduce.2.cloned.1.call-start
  8.0 64.5 %all-gather.4.cloned.1.call-done = f32[6144,128]{1,0:T(8,128)} async-done(((f32[192,128]{1,0:T(8,128)}), f32[6144,128]{1,0:T(8,128)}) %all-gather.4.cloned.1.call-update) | async-done | bytes 3145744 | tf_op jit(solution)/shard_map/all_gather | solution.py:26
  72.4 0.0 copy-done
  72.4 3.9 %fusion.5 = f32[64,128]{1,0:T(8,128)S(1)} fusion(f32[64,6144]{1,0:T(8,128)S(1)} %copy-done, f32[6144,128]{1,0:T(8,128)} %all-gather.4.cloned.1.call-done), kind=kOutput, calls=%fused_computation.14 | convolution fusion | flops 603979776 | bytes 4751360 | tf_op jit(solution)/shard_map/dot_general | solution.py:24
  76.3 0.9 fusion.6
  77.3 0.0 all-reduce.2.cloned.1.call-update
  77.3 0.0 reduce-scatter.4.cloned.1.call-start
  77.3 4.4 %convolution_bitcast_fusion = f32[6144,128]{0,1:T(8,128)} fusion(f32[64,128]{1,0:T(8,128)S(1)} %fusion.5, f32[64,6144]{1,0:T(8,128)S(1)} %copy-done), kind=kOutput, calls=%fused_computation | convolution fusion | flops 603979776 | bytes 4751360 | tf_op jit(solution)/shard_map/dot_general | solution.py:35
  81.7 3.6 copy.10
  85.2 0.0 reduce-scatter.4.cloned.1.call-update
  85.3 0.2 all-gather.6.cloned.1.call-start
  85.5 112.7 %all-reduce.2.cloned.1.call-done = f32[128,128]{0,1:T(8,128)} async-done(((f32[128,128]{0,1:T(8,128)}), f32[128,128]{0,1:T(8,128)}) %all-reduce.2.cloned.1.call-update) | async-done | bytes 65552 | tf_op jit(solution)/shard_map/psum | solution.py:46
  198.2 0.9 copy.8
  199.1 0.9 fusion.4
  200.0 11.7 %cholesky.16 = f32[128,128]{1,0:T(8,128)S(1)} custom-call(f32[128,128]{1,0:T(8,128)S(1)} %fusion.4), custom_call_target="Cholesky" | custom-call | tf_op jit(solution)/shard_map/jit(cholesky)/cholesky | solution.py:47
  211.7 0.6 compare_reduce_fusion
  212.4 0.7 fusion
  213.0 9.8 %custom-call.10 = f32[1,128,128]{1,2,0:T(8,128)S(1)} custom-call(f32[1,128,128]{2,1,0:T(8,128)S(1)} %fusion), custom_call_target="InvertDiagBlocksLowerTriangular" | custom-call | tf_op jit(solution)/shard_map/jit(_solve_triangular)/triangular_solve | solution.py:48
  222.9 80.8 %reduce-scatter.4.cloned.1.call-done = f32[192,128]{1,0:T(8,128)} async-done(((f32[6144,128]{1,0:T(8,128)}), f32[192,128]{1,0:T(8,128)}) %reduce-scatter.4.cloned.1.call-update) | async-done | bytes 98320
  303.6 1.1 fusion.1
  304.8 0.0 copy-start.1
  304.8 1.1 fusion.7
  305.9 0.0 all-gather.6.cloned.1.call-update
  305.9 0.8 convolution_multiply_fusion
  306.7 57.6 %all-gather.6.cloned.1.call-done = f32[4096,128]{1,0:T(8,128)} async-done(((f32[128,128]{1,0:T(8,128)}), f32[4096,128]{1,0:T(8,128)}) %all-gather.6.cloned.1.call-update) | async-done | bytes 2097168 | tf_op jit(solution)/shard_map/all_gather | solution.py:11
  364.2 1.7 reduce_sum.9
  365.9 0.6 broadcast_multiply_fusion
  366.6 0.0 copy-done.1
  (1 shorter events, 0.0 us)
Async XLA Ops:
  7.2 65.3 %copy-start = (f32[64,6144]{1,0:T(8,128)S(1)}, f32[64,6144]{1,0:T(8,128)}, u32[]{:S(2)}) copy-start(f32[64,6144]{1,0:T(8,128)} %param.2) | copy-start | bytes 4718596
  7.2 65.2 %all-gather.4.cloned.1.call-start = ((), (), s32[]{:S(2)}) async-start(), calls=%async_computation.1 | async-start | bytes 3244032 | tf_op jit(solution)/shard_map/all_gather | solution.py:26
  7.9 190.3 %all-reduce.2.cloned.1.call-start = ((), (), s32[]{:S(2)}) async-start(), calls=%async_computation.2 | async-start | bytes 131072 | tf_op jit(solution)/shard_map/psum | solution.py:46
  77.3 226.4 %reduce-scatter.4.cloned.1.call-start = ((), (), s32[]{:S(2)}) async-start(), calls=%async_computation.4 | async-start | bytes 3244032
  85.3 279.0 %all-gather.6.cloned.1.call-start = ((), (), s32[]{:S(2)}) async-start(), calls=%async_computation.3 | async-start | bytes 2162688 | tf_op jit(solution)/shard_map/all_gather | solution.py:11
  304.8 61.8 %copy-start.1 = (f32[128,192]{0,1:T(8,128)}, f32[128,192]{0,1:T(8,128)S(1)}, u32[]{:S(2)}) copy-start(f32[128,192]{0,1:T(8,128)S(1)} %fusion.1) | copy-start | bytes 294916
Sparse Core Ops, SparseCore 0:
  10.9 61.5 all-gather.3
  78.6 119.5 all-reduce.1
  203.6 99.9 reduce-scatter.3
  306.9 57.2 all-gather.5
